TPU v7x, 128 devices: a 2x2x16 block of a 8x8x16 slice. The times are simulated.
128 devices in a mesh: grp: 4 (over x, y), tok: 16 (over z), mdl: 2 (over core).
Axes of the slice: x: 2, y: 2, z: 16, core: 2. Of those that a mesh axis runs over, the one named last changes fastest.
The devices are a block of a 8x8x16 slice.
Arguments:
- hidden: bfloat16 [4096, 4096], P(('grp', 'tok'), 'mdl'), parts along dimension 0, may hold values from -3 to 3
- queries: bfloat16 [4096, 16, 128], P(('grp', 'tok'), 'mdl'), parts along dimension 0, may hold values from -8 to 8
- cache: bfloat16 [64, 2048, 4, 2, 128], P(('grp', 'tok'), None, 'mdl'), parts along dimension 0, may hold values from -8 to 8
- cache_lengths: int32 [64], P(('grp', 'tok')), parts along dimension 0, may hold values from 128 to 2048, as said below
- wkv: bfloat16 [4096, 4, 2, 128], P('tok', 'mdl'), may hold values from -0.09375 to 0.09375
- wo: bfloat16 [16, 128, 4096], P('mdl', None, 'tok'), may hold values from -0.5 to 0.5
- attn_gain: bfloat16 [4096], replicated, may hold values from 0.5 to 1.5
- moe_gain: bfloat16 [4096], replicated, may hold values from 0.5 to 1.5
- w_gate: bfloat16 [32, 4096, 896], P(('tok', 'mdl')), may hold values from -0.09375 to 0.09375
- w_up: bfloat16 [32, 4096, 896], P(('tok', 'mdl')), may hold values from -0.09375 to 0.09375
- w_down: bfloat16 [32, 896, 4096], P(('tok', 'mdl')), may hold values from -0.0625 to 0.0625
- expert_ids: int32 [4096, 2], P(('grp', 'tok', 'mdl')), parts along dimension 0, may hold values from 0 to 3, all different within a row; in each aligned block of 32 rows (0 to 31, 32 to 63, ...) at most 18 rows name the same one
- gates: float32 [4096, 2], P(('grp', 'tok', 'mdl')), parts along dimension 0, may hold values from 0.1 to 1
Outputs:
- mixed: bfloat16 [4096, 4096], P(('grp', 'tok', 'mdl')), parts along dimension 0
- fresh_key_value: bfloat16 [4096, 4, 2, 128], P(('grp', 'tok'), 'mdl'), parts along dimension 0
There are 4 independent parts, one for each index of `grp`. A program takes and returns all parts, laid end to end along the dimension named above; an argument that names none is the same for every part. Nothing has to cross between parts.
Inputs may be any that keep to these rules, and one draw needn't show every extreme that they name: `expert_ids`: each token names 2 different experts; in aligned blocks of 32 rows no expert is named by more than 18 rows, a bound that some block reaches. `cache_lengths`: some rollout holds exactly 2048 cached positions.
All inputs are finite; a program needn't handle non-finite values.
Results may differ from a plain program's by a relative error of at most 0.007.
Values may be sent and summed in bfloat16 or wider, within the bound.
A program may use at most 128 MiB of HBM per device.

v0:
```python
import math
import jax
import jax.numpy as jnp
from jax import lax
from jax.sharding import PartitionSpec as P

EXPERTS = 4
TOPK = 2
eps_norm = 1e-05
rope_base = 1000000.0
mask_fill = -1e30


def joined_along(tiles, dim):
    dims = list(tiles.shape[1:])
    dims[dim] *= tiles.shape[0]
    return jnp.moveaxis(tiles, 0, dim).reshape(dims)


def sent_to_all(shard, axis):
    copies = jnp.broadcast_to(shard, (lax.axis_size(axis), *shard.shape))
    return lax.all_to_all(copies, axis, split_axis=0, concat_axis=0, tiled=True)


def collect(shard, axis, dim):
    return joined_along(sent_to_all(shard, axis), dim)


def in_blocks(shard, dim, size):
    dims = shard.shape
    tiles = shard.reshape(*dims[:dim], size, dims[dim] // size, *dims[dim + 1 :])
    return jnp.moveaxis(tiles, dim, 0)


def sent_and_summed(shard, axis, dim):
    tiles = in_blocks(shard, dim, lax.axis_size(axis))
    arrived = lax.all_to_all(tiles, axis, split_axis=0, concat_axis=0, tiled=True)
    return arrived.sum(axis=0)


def sent_and_summed_2(shard, axis, dim):
    size = lax.axis_size(axis)
    tiles = lax.all_to_all(in_blocks(shard, dim, size), axis, 0, 0, tiled=True)
    return jnp.sum(tiles.astype(jnp.float32), axis=0)


def rms_scale(values_in, gain):
    values = values_in.astype(jnp.float32)
    meansq = jnp.mean(values * values, axis=-1, keepdims=True)
    return values * lax.rsqrt(meansq + eps_norm) * gain.astype(jnp.float32)


def rotate(key_rows, positions):
    half_dim = key_rows.shape[-1] // 2
    inverse = jnp.exp(
        jnp.arange(half_dim, dtype=jnp.float32) * (-2.0 * math.log(rope_base) / key_rows.shape[-1])
    )
    angle = positions.astype(jnp.float32)[:, None] * inverse[None, :]
    cosine = jnp.cos(angle)[:, None, :]
    sine_vals = jnp.sin(angle)[:, None, :]
    front_half = key_rows[..., :half_dim]
    back_half = key_rows[..., half_dim:]
    return jnp.concatenate(
        [front_half * cosine - back_half * sine_vals, back_half * cosine + front_half * sine_vals],
        axis=-1,
    )


def score_rows(query_rows, key_rows, scale_factor):
    return (
        lax.dot_general(
            query_rows, key_rows, (((1,), (1,)), ((), ())), preferred_element_type=jnp.float32
        )
        * scale_factor
    )


def head_attention(query_rows, cache_keys, cache_values, length, new_keys, new_values, head_group):
    row_count = query_rows.shape[0]
    block_len = min(512, cache_keys.shape[0])
    scale_factor = 1.0 / math.sqrt(query_rows.shape[1])
    token_of_row = jnp.arange(row_count) // head_group
    block_total = (length + block_len - 1) // block_len

    def block_scores(block_idx):
        row_offset = block_idx * block_len
        block_keys = lax.dynamic_slice_in_dim(cache_keys, row_offset, block_len, 0)
        allowed = row_offset + jnp.arange(block_len) < length
        return (
            jnp.where(
                allowed[None, :], score_rows(query_rows, block_keys, scale_factor), mask_fill
            ),
            allowed,
        )

    new_allowed = jnp.arange(new_keys.shape[0])[None, :] <= token_of_row[:, None]
    new_scores = jnp.where(new_allowed, score_rows(query_rows, new_keys, scale_factor), mask_fill)
    first_max = jnp.max(new_scores, axis=1)
    first_sum = jnp.sum(
        jnp.where(new_allowed, jnp.exp(new_scores - first_max[:, None]), 0.0), axis=1
    )

    def first_pass(block_idx, carry):
        run_max, run_sum = carry
        scores, allowed = block_scores(block_idx)
        next_max = jnp.maximum(run_max, jnp.max(scores, axis=1))
        weights = jnp.where(allowed[None, :], jnp.exp(scores - next_max[:, None]), 0.0)
        return (next_max, run_sum * jnp.exp(run_max - next_max) + jnp.sum(weights, axis=1))

    row_max, row_sum = lax.fori_loop(0, block_total, first_pass, (first_max, first_sum))
    new_probs = (
        jnp.where(new_allowed, jnp.exp(new_scores - row_max[:, None]), 0.0) / row_sum[:, None]
    ).astype(jnp.bfloat16)
    start_total = jnp.dot(new_probs, new_values, preferred_element_type=jnp.float32)

    def second_pass(block_idx, total):
        scores, allowed = block_scores(block_idx)
        probs = (
            jnp.where(allowed[None, :], jnp.exp(scores - row_max[:, None]), 0.0) / row_sum[:, None]
        ).astype(jnp.bfloat16)
        block_values = lax.dynamic_slice_in_dim(cache_values, block_idx * block_len, block_len, 0)
        return total + jnp.dot(probs, block_values, preferred_element_type=jnp.float32)

    total = lax.fori_loop(0, block_total, second_pass, start_total)
    return total.astype(jnp.bfloat16)


def shards(
    hidden,
    queries,
    cache,
    cache_lengths,
    wkv,
    wo,
    attn_gain,
    moe_gain,
    w_gate,
    w_up,
    w_down,
    expert_ids,
    gates,
):
    full_rows = collect(hidden, "mdl", 1)
    span_len = full_rows.shape[0]
    normalized_input = rms_scale(full_rows, attn_gain).astype(jnp.bfloat16)
    kv_heads = wkv.shape[1]
    head_dim = wkv.shape[3]
    weight_piece = lax.all_gather(wkv, "tok", axis=0, tiled=True)
    key_value_projection = jnp.dot(
        normalized_input,
        weight_piece.reshape(weight_piece.shape[0], -1),
        preferred_element_type=jnp.float32,
    ).reshape(span_len, kv_heads, 2, head_dim)
    length = cache_lengths[0]
    positions = length + jnp.arange(span_len, dtype=jnp.int32)
    fresh_key_value = jnp.stack(
        [rotate(key_value_projection[:, :, 0], positions), key_value_projection[:, :, 1]], axis=2
    ).astype(jnp.bfloat16)
    head_group = queries.shape[1] // kv_heads
    outputs = []
    for head_index in range(kv_heads):
        query_rows = queries[:, head_index * head_group : (head_index + 1) * head_group].reshape(
            span_len * head_group, head_dim
        )
        attended = head_attention(
            query_rows,
            cache[0, :, head_index, 0],
            cache[0, :, head_index, 1],
            length,
            fresh_key_value[:, head_index, 0],
            fresh_key_value[:, head_index, 1],
            head_group,
        )
        outputs.append(attended.reshape(span_len, head_group * head_dim))
    heads_out = jnp.concatenate(outputs, axis=1)
    weight_piece = lax.all_gather(wo, "tok", axis=2, tiled=True)
    attn_out = jnp.dot(
        heads_out,
        weight_piece.reshape(-1, weight_piece.shape[2]),
        preferred_element_type=jnp.float32,
    )
    core_rows = span_len // lax.axis_size("mdl")
    core_start = lax.axis_index("mdl") * core_rows
    attn_rows = sent_and_summed(attn_out, "mdl", 0)
    resid = (
        lax.dynamic_slice_in_dim(full_rows, core_start, core_rows, 0).astype(jnp.float32)
        + attn_rows
    )
    moe_in = rms_scale(resid, moe_gain).astype(jnp.bfloat16)
    expert_range = jnp.arange(EXPERTS)
    matches = expert_ids[:, :, None] == expert_range[None, None, :]
    chosen = jnp.sum(matches.astype(jnp.int32), axis=1)
    route = jnp.sum(jnp.where(matches, gates[:, :, None], 0.0), axis=1)
    slot_of = jnp.cumsum(chosen, axis=0) - chosen
    capacity = core_rows * TOPK * 9 // (8 * EXPERTS)
    slot_range = jnp.arange(capacity)
    select = (slot_of.T[:, None, :] == slot_range[None, :, None]) & (chosen.T[:, None, :] > 0)
    send_rows = jnp.einsum(
        "eci,id->ecd", select.astype(jnp.bfloat16), moe_in, preferred_element_type=jnp.float32
    ).astype(jnp.bfloat16)
    owners = lax.axis_size("tok") * lax.axis_size("mdl")
    slabs = owners // EXPERTS
    model_width = moe_in.shape[1]
    core_count = lax.axis_size("mdl")
    send_chip = jnp.repeat(send_rows, slabs // core_count, axis=0)
    received = lax.all_to_all(send_chip, "tok", split_axis=0, concat_axis=0, tiled=True)
    chip_count = received.shape[0]
    item_count = received.shape[1]
    both_cores = collect(received[:, None], "mdl", 1)
    received = both_cores.reshape(-1, item_count, model_width)
    flat_rows = received.reshape(-1, model_width)
    gate_val = jnp.dot(flat_rows, w_gate[0], preferred_element_type=jnp.float32)
    up_val = jnp.dot(flat_rows, w_up[0], preferred_element_type=jnp.float32)
    slab_hidden = (jax.nn.silu(gate_val) * up_val).astype(jnp.bfloat16)
    slab_out = jnp.dot(slab_hidden, w_down[0], preferred_element_type=jnp.float32).astype(
        jnp.bfloat16
    )
    slab_out = slab_out.reshape(received.shape)
    per_core = slab_out.reshape(chip_count, core_count, item_count, model_width).astype(jnp.float32)
    chip_total = sent_and_summed_2(per_core.astype(jnp.bfloat16), "mdl", 1)
    returned = lax.all_to_all(
        chip_total[:, 0].astype(jnp.bfloat16), "tok", split_axis=0, concat_axis=0, tiled=True
    ).astype(jnp.float32)
    summed = jnp.sum(returned.reshape(EXPERTS, slabs // core_count, capacity, model_width), axis=1)
    weight_table = select.astype(jnp.float32) * route.T[:, None, :]
    moe_out = jnp.einsum("eci,ecd->id", weight_table, summed, precision=lax.Precision.HIGHEST)
    mixed = (resid + moe_out).astype(jnp.bfloat16)
    return (mixed, fresh_key_value)


def solution(mesh):
    in_specs = (
        P(("grp", "tok"), "mdl"),
        P(("grp", "tok"), "mdl", None),
        P(("grp", "tok"), None, "mdl", None, None),
        P(("grp", "tok")),
        P("tok", "mdl", None, None),
        P("mdl", None, "tok"),
        P(),
        P(),
        P(("tok", "mdl"), None, None),
        P(("tok", "mdl"), None, None),
        P(("tok", "mdl"), None, None),
        P(("grp", "tok", "mdl"), None),
        P(("grp", "tok", "mdl"), None),
    )
    out_specs = (P(("grp", "tok", "mdl"), None), P(("grp", "tok"), "mdl", None, None))
    return jax.shard_map(shards, mesh=mesh, in_specs=in_specs, out_specs=out_specs, check_vma=False)
```

profile of v0, /device:TPU:84, one launch (start us, length us, event | category | flops | bytes accessed | tf_op | source)
XLA Modules:
  0.0 608.0 jit_solution(13349930791535107725)
XLA Ops:
  8.1 0.7 all-gather.5.cloned.1.call-update
  8.8 1.8 broadcast_in_dim.140
  10.6 3.5 all-to-all-start
  16.9 1.2 reshape.194
  18.7 3.0 fusion.112
  21.7 0.9 copy_bitcast_fusion.2
  22.8 67.3 %all-gather.3.cloned.1.call-done = bf16[4096,2,2,128]{3,2,1,0:T(2,128)(2,1)} async-done(((bf16[256,2,2,128]{3,2,1,0:T(2,128)(2,1)}), bf16[4096,2,2,128]{3,2,1,0:T(2,128)(2,1)}) %all-gather.3.cloned.1.call-update) | async-done | bytes 4194320 | tf_op jit(solution)/shard_map/all_gather | solution.py:148
  90.1 11.2 %copy.122 = bf16[4096,2,2,128]{0,3,2,1:T(8,128)(2,1)} copy(bf16[4096,2,2,128]{3,2,1,0:T(2,128)(2,1)} %all-gather.3.cloned.1.call-done) | data formatting | bytes 8388608 | tf_op jit(solution)/shard_map/reshape | solution.py:151
  101.2 3.7 fusion.116
  105.5 1.1 while.44
  106.9 2.1 while.45
  107.6 1.4 fusion.144
  109.1 1.1 while.46
  110.5 1.2 while.47
  111.8 101.1 %all-gather.5.cloned.1.call-done = bf16[8,128,4096]{2,1,0:T(8,128)(2,1)} async-done(((bf16[8,128,256]{2,1,0:T(8,128)(2,1)}), bf16[8,128,4096]{2,1,0:T(8,128)(2,1)}) %all-gather.5.cloned.1.call-update) | async-done | bytes 8388624 | tf_op jit(solution)/shard_map/all_gather | solution.py:176
  212.9 5.0 fusion.80
  217.9 4.6 all_to_all.30
  223.7 149.6 %all_to_all.31 = bf16[16,18,4096]{2,1,0:T(8,128)(2,1)S(1)} all-to-all(bf16[16,18,4096]{2,1,0:T(8,128)(2,1)S(1)} %bitcast.122), channel_id=1, replica_groups=mesh['grp'=4,'tok'=16,'mdl'=2] {'tok'}, dimensions={0} | all-to-all | bytes 4718592 | tf_op jit(solution)/shard_map/all_to_all | solution.py:206
  373.3 1.3 copy.114
  375.2 7.7 %all_to_all.32 = bf16[2,16,1,18,4096]{4,1,3,2,0:T(8,128)(2,1)S(1)} all-to-all(bf16[2,16,1,18,4096]{4,1,3,2,0:T(8,128)(2,1)S(1)} %broadcast_in_dim.146), channel_id=1, replica_groups=mesh['grp'=4,'tok'=16,'mdl'=2] {'mdl'}, dimensions={0} | all-to-all | bytes 9437184 | tf_op jit(solution)/shard_map/all_to_all | solution.py:22
  382.9 5.4 copy.115
  388.3 7.8 %reshape_reshape_reshape.3 = bf16[576,4096]{1,0:T(8,128)(2,1)} reshape(bf16[16,2,1,18,4096]{4,3,1,0,2:T(8,128)(2,1)} %copy.115) | data formatting | bytes 9437184 | tf_op jit(solution)/shard_map/reshape;reshape;reshape | solution.py:211
  396.1 10.7 %fusion.54 = f32[576,896]{1,0:T(8,128)S(1)} fusion(bf16[576,4096]{1,0:T(8,128)(2,1)} %reshape_reshape_reshape.3, bf16[1,4096,896]{2,1,0:T(8,128)(2,1)} %param.29), kind=kOutput, calls=%fused_computation.62 | convolution fusion | flops 4227858432 | bytes 14123008 | tf_op jit(solution)/shard_map/dot_general | solution.py:212
  406.8 17.4 %fusion.56 = bf16[576,4096]{1,0:T(8,128)(2,1)} fusion(bf16[1,896,4096]{2,1,0:T(8,128)(2,1)} %param.31, f32[576,896]{1,0:T(8,128)S(1)} %fusion.54, bf16[576,4096]{1,0:T(8,128)(2,1)} %reshape_reshape_reshape.3, bf16[1,4096,896]{2,1,0:T(8,128)(2,1)} %param.30), kind=kOutput, calls=%fused_computation.65 | convolution fusion | flops 8461172736 | bytes 26181632 | tf_op jit(solution)/shard_map/dot_general | solution.py:215
  424.2 7.6 %reshape.188 = bf16[16,2,1,18,4096]{4,3,1,0,2:T(8,128)(2,1)} reshape(bf16[576,4096]{1,0:T(8,128)(2,1)} %fusion.56) | data formatting | bytes 9437184 | tf_op jit(solution)/shard_map/reshape | solution.py:31
  431.8 5.4 copy.116
  437.2 8.6 %all_to_all.33 = bf16[2,16,1,18,4096]{4,1,3,2,0:T(8,128)(2,1)} all-to-all(bf16[2,16,1,18,4096]{4,1,3,2,0:T(8,128)(2,1)S(1)} %copy.116), channel_id=1, replica_groups=mesh['grp'=4,'tok'=16,'mdl'=2] {'mdl'}, dimensions={0} | all-to-all | bytes 9437184 | tf_op jit(solution)/shard_map/all_to_all | solution.py:43
  445.8 3.6 reduce_sum.109
  449.4 3.1 copy.117
  452.5 6.5 %all-to-all-start.5 = ((bf16[16,18,4096]{2,1,0:T(8,128)(2,1)}), bf16[16,18,4096]{2,1,0:T(8,128)(2,1)S(1)}, u32[]{:S(2)}, u32[]{:S(2)}) async-start(bf16[16,18,4096]{2,1,0:T(8,128)(2,1)} %copy.117), calls=%async_computation.5 | async-start | bytes 6291456 | tf_op jit(solution)/shard_map/all_to_all | solution.py:221
  459.8 138.6 %all-to-all-done.5 = bf16[16,18,4096]{2,1,0:T(8,128)(2,1)S(1)} async-done(((bf16[16,18,4096]{2,1,0:T(8,128)(2,1)}), bf16[16,18,4096]{2,1,0:T(8,128)(2,1)S(1)}, u32[]{:S(2)}, u32[]{:S(2)}) %all-to-all-start.5) | async-done | bytes 2359328 | tf_op jit(solution)/shard_map/all_to_all | solution.py:221
  599.6 1.6 fusion.60
  (81 shorter events, 12.4 us)
Async XLA Ops:
  7.2 10.9 %copy-start.8 = (s32[32,2]{0,1:T(2,128)S(1)}, s32[32,2]{0,1:T(2,128)}, u32[]{:S(2)}) copy-start(s32[32,2]{0,1:T(2,128)} %param.32) | copy-start | bytes 772
  7.2 11.2 %copy-start.7 = (bf16[4096]{0:T(1024)(128)(2,1)S(1)}, bf16[4096]{0:T(1024)(128)(2,1)}, u32[]{:S(2)}) copy-start(bf16[4096]{0:T(1024)(128)(2,1)} %param.28) | copy-start | bytes 24580
  7.2 11.4 %copy-start.6 = (bf16[64,8,128]{2,1,0:T(8,128)(2,1)S(1)}, bf16[64,8,128]{2,1,0:T(8,128)(2,1)}, u32[]{:S(2)}) copy-start(bf16[64,8,128]{2,1,0:T(8,128)(2,1)} %param.22) | copy-start | bytes 393220
  7.2 11.5 %copy-start.2 = (bf16[1,2048,2,2,128]{4,3,2,1,0:T(2,128)(2,1)S(1)}, bf16[1,2048,2,2,128]{4,3,2,1,0:T(2,128)(2,1)}, u32[]{:S(2)}) copy-start(bf16[1,2048,2,2,128]{4,3,2,1,0:T(2,128)(2,1)} %param.23) | copy-start | bytes 6291460
  7.2 82.8 %all-gather.3.cloned.1.call-start = ((), (), s32[]{:S(2)}) async-start(), calls=%async_computation.6 | async-start | bytes 4456448 | tf_op jit(solution)/shard_map/all_gather | solution.py:148
  8.0 204.9 %all-gather.5.cloned.1.call-start = ((), (), s32[]{:S(2)}) async-start(), calls=%async_computation.7 | async-start | bytes 8912896 | tf_op jit(solution)/shard_map/all_gather | solution.py:176
  10.6 5.2 all-to-all-start
  18.1 204.7 %copy-start.3 = (bf16[2,8,8,2048]{3,2,0,1:T(8,128)(2,1)}, bf16[2,8,8,2048]{3,2,0,1:T(8,128)(2,1)S(1)}, u32[]{:S(2)}) copy-start(bf16[2,8,8,2048]{3,2,0,1:T(8,128)(2,1)S(1)} %copy.129) | copy-start | bytes 1572868
  22.8 78.5 %copy-start.5 = (bf16[64,4096,1,1]{1,0,2,3:T(8,128)(2,1)S(1)}, bf16[64,4096,1,1]{1,0,2,3:T(8,128)(2,1)}, u32[]{:S(2)}) copy-start(bf16[64,4096,1,1]{1,0,2,3:T(8,128)(2,1)} %reshape.194) | copy-start | bytes 1572868
  222.6 150.7 %copy-start = (f32[32,4096]{1,0:T(8,128)}, f32[32,4096]{1,0:T(8,128)S(1)}, u32[]{:S(2)}) copy-start(f32[32,4096]{1,0:T(8,128)S(1)} %reduce_sum.105) | copy-start | bytes 1572868
  449.4 9.6 %copy-start.9 = (f32[32,2]{0,1:T(2,128)S(1)}, f32[32,2]{0,1:T(2,128)}, u32[]{:S(2)}) copy-start(f32[32,2]{0,1:T(2,128)} %param.33) | copy-start | bytes 772
  452.5 145.9 %all-to-all-start.5 = ((bf16[16,18,4096]{2,1,0:T(8,128)(2,1)}), bf16[16,18,4096]{2,1,0:T(8,128)(2,1)S(1)}, u32[]{:S(2)}, u32[]{:S(2)}) async-start(bf16[16,18,4096]{2,1,0:T(8,128)(2,1)} %copy.117), calls=%async_computation.5 | async-start | bytes 6291456 | tf_op jit(solution)/shard_map/all_to_all | solution.py:221
  598.4 1.0 copy-start.1
  598.4 1.2 copy-start.4
Sparse Core Ops, SparseCore 0:
  9.7 80.3 all-gather.2
  91.7 121.2 all-gather.4
where the time goes:
time: 609 us; the launch traced here: 608 us
  waiting for transfers between devices  309 us (51%)
  blocking collectives  171 us (28%)
  local copies, waits for them, and re-layouts  52.8 us (9%)
  matrix products  42.1 us (7%)
  between operations  15.1 us (2%)
  starting transfers between devices  10.2 us (2%)
  other arithmetic  8.38 us (1%)
    all_to_all x1, blocking collectives, shards(): lax.all_to_all(send_chip, 'tok', split_axis=0, concat_axis=0, tiled=True)  150 us
    all_to_all x1, waiting for transfers between devices, shards(): lax.all_to_all(chip_total[:, 0].astype(jnp.bfloat16), 'tok', split_axis=0...  139 us
    all_gather x1, waiting for transfers between devices, shards(): weight_piece = lax.all_gather(wo, 'tok', axis=2, tiled=True)  101 us
    all_gather x1, waiting for transfers between devices, shards(): weight_piece = lax.all_gather(wkv, 'tok', axis=0, tiled=True)  67.3 us
    dot_general x1, matrix products, shards(): jnp.dot(slab_hidden, w_down[0], preferred_element_type=jnp.float32)  17.4 us
  transfers between devices with their start and end apart: 4, of which 4 were waited for; matrix products, arithmetic and copies ran while one was open for 5% of the time, Pallas kernels for 0%

commit v1 on v0

--- a/solution.py
+++ b/solution.py
@@ -173,7 +173,9 @@
         )
         outputs.append(attended.reshape(span_len, head_group * head_dim))
     heads_out = jnp.concatenate(outputs, axis=1)
-    weight_piece = lax.all_gather(wo, "tok", axis=2, tiled=True)
+    weight_piece = jnp.concatenate(
+        lax.all_to_all(jnp.stack([wo] * lax.axis_size("tok")), "tok", 0, 0), axis=2
+    )
     attn_out = jnp.dot(
         heads_out,
         weight_piece.reshape(-1, weight_piece.shape[2]),

time: 609 us -> 870 us (1.43)
  waiting for transfers between devices: 309 us -> 513 us
  local copies, waits for them, and re-layouts: 52.8 us -> 82.1 us
  starting transfers between devices: 10.2 us -> 23.7 us
    all_gather x1, waiting for transfers between devices: 67.3 us -> 345 us  [shards(): weight_piece = lax.all_gather(wkv, 'tok', axis=0, tiled=True)]
    all_gather x1 -> x0, waiting for transfers between devices: 101 us -> none  [shards(): weight_piece = lax.all_gather(wo, 'tok', axis=2, tiled=True)]
    all_to_all x1, waiting for transfers between devices: 0.34 us -> 28.5 us  [shards(): lax.all_to_all(jnp.stack([wo] * lax.axis_size('tok')), 'tok', 0, 0)]
    another operation x0 -> x2, local copies, waits for them, and re-layouts: none -> 18.8 us  [the longest x1 13.5 us: shards(): weight_piece.reshape(-1, weight_piece.shape[2])]
    all_to_all x1, starting transfers between devices: 3.52 us -> 17.2 us  [shards(): lax.all_to_all(jnp.stack([wo] * lax.axis_size('tok')), 'tok', 0, 0)]
    reshape x0 -> x1, local copies, waits for them, and re-layouts: none -> 11.8 us  [shards(): jnp.concatenate(lax.all_to_all(jnp.stack([wo] * lax.axis_size('tok')), 't...]
  transfers between devices with their start and end apart: 4 -> 3, of which waited for: 4 -> 3; matrix products, arithmetic and copies ran while one was open for 5% -> 3% of each run, Pallas kernels for 0% -> 0%
where the time goes in v1:
time: 870 us; the launch traced here: 862 us
  waiting for transfers between devices  513 us (59%)
  blocking collectives  177 us (20%)
  local copies, waits for them, and re-layouts  82.1 us (9%)
  matrix products  42 us (5%)
  starting transfers between devices  23.7 us (3%)
  between operations  15.3 us (2%)
    all_gather x1, waiting for transfers between devices, shards(): weight_piece = lax.all_gather(wkv, 'tok', axis=0, tiled=True)  345 us
    all_to_all x1, blocking collectives, shards(): lax.all_to_all(send_chip, 'tok', split_axis=0, concat_axis=0, tiled=True)  152 us
    all_to_all x1, waiting for transfers between devices, shards(): lax.all_to_all(chip_total[:, 0].astype(jnp.bfloat16), 'tok', split_axis=0...  139 us
    all_to_all x1, waiting for transfers between devices, shards(): lax.all_to_all(jnp.stack([wo] * lax.axis_size('tok')), 'tok', 0, 0)  28.5 us
    dot_general x1, matrix products, shards(): jnp.dot(slab_hidden, w_down[0], preferred_element_type=jnp.float32)  17.4 us
  transfers between devices with their start and end apart: 3, of which 3 were waited for; matrix products, arithmetic and copies ran while one was open for 3% of the time, Pallas kernels for 0%

profile of v1, /device:TPU:84, one launch (start us, length us, event | category | flops | bytes accessed | tf_op | source)
XLA Modules:
  0.0 862.4 jit_solution(16127130322035127063)
XLA Ops:
  8.2 4.2 all_to_all.35
  12.3 5.3 stack.9
  17.7 17.2 %all-to-all-start.1 = ((bf16[16,8,128,256]{3,2,1,0:T(8,128)(2,1)}), bf16[16,8,128,256]{3,2,1,0:T(8,128)(2,1)}, u32[]{:S(2)}, u32[]{:S(2)}) async-start(bf16[16,8,128,256]{3,2,1,0:T(8,128)(2,1)} %stack.9), calls=%async_computation.1 | async-start | bytes 16777216 | tf_op jit(solution)/shard_map/all_to_all | solution.py:177
  37.4 1.2 reshape.196
  39.2 3.0 fusion.112
  43.3 345.2 %all-gather.2.cloned.1.call-done = bf16[4096,2,2,128]{3,2,1,0:T(2,128)(2,1)} async-done(((bf16[256,2,2,128]{3,2,1,0:T(2,128)(2,1)}), bf16[4096,2,2,128]{3,2,1,0:T(2,128)(2,1)}) %all-gather.2.cloned.1.call-update) | async-done | bytes 4194320 | tf_op jit(solution)/shard_map/all_gather | solution.py:148
  388.5 11.2 %copy.127 = bf16[4096,2,2,128]{0,3,2,1:T(8,128)(2,1)} copy(bf16[4096,2,2,128]{3,2,1,0:T(2,128)(2,1)} %all-gather.2.cloned.1.call-done) | data formatting | bytes 8388608 | tf_op jit(solution)/shard_map/reshape | solution.py:151
  399.8 3.6 fusion.116
  405.3 2.1 while.47
  406.0 1.4 fusion.150
  407.5 1.1 while.44
  408.9 1.7 while.45
  410.7 28.5 %all-to-all-done.1 = bf16[16,8,128,256]{3,2,1,0:T(8,128)(2,1)} async-done(((bf16[16,8,128,256]{3,2,1,0:T(8,128)(2,1)}), bf16[16,8,128,256]{3,2,1,0:T(8,128)(2,1)}, u32[]{:S(2)}, u32[]{:S(2)}) %all-to-all-start.1) | async-done | bytes 8388640 | tf_op jit(solution)/shard_map/all_to_all | solution.py:177
  439.2 11.8 %copy.115 = bf16[8,128,16,256]{3,2,1,0:T(8,128)(2,1)} copy(bf16[8,128,16,256]{3,1,0,2:T(8,128)(2,1)} %bitcast.20) | data formatting | bytes 16777216 | tf_op jit(solution)/shard_map/reshape | solution.py:176
  451.0 13.5 %reshape.197 = bf16[1024,4096,1]{1,0,2:T(8,128)(2,1)} reshape(bf16[8,128,16,256]{3,2,1,0:T(8,128)(2,1)} %copy.115) | data formatting | bytes 16777216 | tf_op jit(solution)/shard_map/reshape;reshape | solution.py:181
  464.4 5.0 fusion.80
  469.4 4.6 all_to_all.36
  475.2 152.1 %all_to_all.37 = bf16[16,18,4096]{2,1,0:T(8,128)(2,1)S(1)} all-to-all(bf16[16,18,4096]{2,1,0:T(8,128)(2,1)S(1)} %bitcast.122), channel_id=1, replica_groups=mesh['grp'=4,'tok'=16,'mdl'=2] {'tok'}, dimensions={0} | all-to-all | bytes 4718592 | tf_op jit(solution)/shard_map/all_to_all | solution.py:208
  627.3 1.3 copy.119
  629.2 7.7 all_to_all.38
  636.9 5.4 copy.120
  642.3 7.8 reshape_reshape_reshape.3
  650.1 10.7 %fusion.54 = f32[576,896]{1,0:T(8,128)S(1)} fusion(bf16[576,4096]{1,0:T(8,128)(2,1)} %reshape_reshape_reshape.3, bf16[1,4096,896]{2,1,0:T(8,128)(2,1)} %param.29), kind=kOutput, calls=%fused_computation.62 | convolution fusion | flops 4227858432 | bytes 14123008 | tf_op jit(solution)/shard_map/dot_general | solution.py:214
  660.8 17.4 %fusion.56 = bf16[576,4096]{1,0:T(8,128)(2,1)} fusion(bf16[1,896,4096]{2,1,0:T(8,128)(2,1)} %param.31, f32[576,896]{1,0:T(8,128)S(1)} %fusion.54, bf16[576,4096]{1,0:T(8,128)(2,1)} %reshape_reshape_reshape.3, bf16[1,4096,896]{2,1,0:T(8,128)(2,1)} %param.30), kind=kOutput, calls=%fused_computation.65 | convolution fusion | flops 8461172736 | bytes 26181632 | tf_op jit(solution)/shard_map/dot_general | solution.py:217
  678.2 7.8 reshape.190
  686.0 5.4 copy.121
  691.4 8.6 %all_to_all.39 = bf16[2,16,1,18,4096]{4,1,3,2,0:T(8,128)(2,1)} all-to-all(bf16[2,16,1,18,4096]{4,1,3,2,0:T(8,128)(2,1)S(1)} %copy.121), channel_id=1, replica_groups=mesh['grp'=4,'tok'=16,'mdl'=2] {'mdl'}, dimensions={0} | all-to-all | bytes 9437184 | tf_op jit(solution)/shard_map/all_to_all | solution.py:43
  700.0 3.6 reduce_sum.109
  703.6 3.1 copy.122
  706.7 6.5 all-to-all-start.6
  713.9 138.6 %all-to-all-done.6 = bf16[16,18,4096]{2,1,0:T(8,128)(2,1)S(1)} async-done(((bf16[16,18,4096]{2,1,0:T(8,128)(2,1)}), bf16[16,18,4096]{2,1,0:T(8,128)(2,1)S(1)}, u32[]{:S(2)}, u32[]{:S(2)}) %all-to-all-start.6) | async-done | bytes 2359328 | tf_op jit(solution)/shard_map/all_to_all | solution.py:223
  853.7 1.6 fusion.60
  (84 shorter events, 14.4 us)
Async XLA Ops:
  17.7 18.7 %copy-start.7 = (bf16[4096]{0:T(1024)(128)(2,1)S(1)}, bf16[4096]{0:T(1024)(128)(2,1)}, u32[]{:S(2)}) copy-start(bf16[4096]{0:T(1024)(128)(2,1)} %param.28) | copy-start | bytes 24580
  17.7 18.7 %copy-start.8 = (bf16[4096]{0:T(1024)(128)(2,1)S(1)}, bf16[4096]{0:T(1024)(128)(2,1)}, u32[]{:S(2)}) copy-start(bf16[4096]{0:T(1024)(128)(2,1)} %param.27) | copy-start | bytes 24580
  17.7 421.5 %all-to-all-start.1 = ((bf16[16,8,128,256]{3,2,1,0:T(8,128)(2,1)}), bf16[16,8,128,256]{3,2,1,0:T(8,128)(2,1)}, u32[]{:S(2)}, u32[]{:S(2)}) async-start(bf16[16,8,128,256]{3,2,1,0:T(8,128)(2,1)} %stack.9), calls=%async_computation.1 | async-start | bytes 16777216 | tf_op jit(solution)/shard_map/all_to_all | solution.py:177
  34.9 3.8 copy-start.9
  34.9 4.2 copy-start.6
  34.9 4.3 copy-start.2
  34.9 353.7 %all-gather.2.cloned.1.call-start = ((), (), s32[]{:S(2)}) async-start(), calls=%async_computation.7 | async-start | bytes 4456448 | tf_op jit(solution)/shard_map/all_gather | solution.py:148
  38.6 435.8 %copy-start.3 = (bf16[2,8,8,2048]{3,2,0,1:T(8,128)(2,1)}, bf16[2,8,8,2048]{3,2,0,1:T(8,128)(2,1)S(1)}, u32[]{:S(2)}) copy-start(bf16[2,8,8,2048]{3,2,0,1:T(8,128)(2,1)S(1)} %copy.134) | copy-start | bytes 1572868
  43.3 356.5 %copy-start.5 = (bf16[64,4096,1,1]{1,0,2,3:T(8,128)(2,1)S(1)}, bf16[64,4096,1,1]{1,0,2,3:T(8,128)(2,1)}, u32[]{:S(2)}) copy-start(bf16[64,4096,1,1]{1,0,2,3:T(8,128)(2,1)} %reshape.196) | copy-start | bytes 1572868
  474.1 153.1 %copy-start = (f32[32,4096]{1,0:T(8,128)}, f32[32,4096]{1,0:T(8,128)S(1)}, u32[]{:S(2)}) copy-start(f32[32,4096]{1,0:T(8,128)S(1)} %reduce_sum.105) | copy-start | bytes 1572868
  703.6 9.6 %copy-start.10 = (f32[32,2]{0,1:T(2,128)S(1)}, f32[32,2]{0,1:T(2,128)}, u32[]{:S(2)}) copy-start(f32[32,2]{0,1:T(2,128)} %param.33) | copy-start | bytes 772
  706.7 145.9 %all-to-all-start.6 = ((bf16[16,18,4096]{2,1,0:T(8,128)(2,1)}), bf16[16,18,4096]{2,1,0:T(8,128)(2,1)S(1)}, u32[]{:S(2)}, u32[]{:S(2)}) async-start(bf16[16,18,4096]{2,1,0:T(8,128)(2,1)} %copy.122), calls=%async_computation.6 | async-start | bytes 6291456 | tf_op jit(solution)/shard_map/all_to_all | solution.py:223
  852.5 1.0 copy-start.1
  852.5 1.2 copy-start.4
Sparse Core Ops, SparseCore 0:
  37.4 351.1 all-gather.1
